TPU v7x, 16 devices: a 4x2x1 block of a 4x4x8 slice. The times are simulated.
16 devices in a mesh: dp: 2 (over y, z), ep: 8 (over x, core).
Axes of the slice: x: 4, y: 2, z: 1, core: 2. Of those that a mesh axis runs over, the one named last changes fastest.
The devices are a block of a 4x4x8 slice.
Arguments:
- tokens: bfloat16 [1024, 2048], P(('dp', 'ep')), parts along dimension 0
- route_idx: int32 [1024, 8], P(('dp', 'ep')), parts along dimension 0
- gate_vals: float32 [1024, 8], P(('dp', 'ep')), parts along dimension 0
- w_gate: bfloat16 [64, 2048, 1024], P('ep')
- w_up: bfloat16 [64, 2048, 1024], P('ep')
- w_down: bfloat16 [64, 1024, 2048], P('ep')
Outputs:
- output: bfloat16 [1024, 2048], P(('dp', 'ep')), parts along dimension 0
There are 2 independent parts. A program takes and returns all parts, laid end to end along the dimension named above; an argument that names none is the same for every part.
All inputs are finite; a program needn't handle non-finite values.
Results may differ from a plain program's by a relative error of at most 0.00782637.
Values are sent between devices in bfloat16 or wider.
A program may use at most 768 MiB of HBM per device.

v0:
```python
import jax
import jax.numpy as jnp
from jax import lax
from jax.sharding import PartitionSpec as P


def pack_index(route_loc, n_experts, capacity):
    hit_mask = route_loc[:, :, None] == jnp.arange(n_experts)
    member = jnp.sum(hit_mask, axis=1, dtype=jnp.int32)
    running = jnp.cumsum(member, axis=0)
    targets = jnp.arange(capacity) + 1
    row_ids = jax.vmap(lambda column: jnp.searchsorted(column, targets, side="left"), in_axes=1)(running)
    slot_pos = jnp.take_along_axis(running, route_loc, axis=1) - 1
    return row_ids, slot_pos


def combine_rows(returned, flat_pos, gate_loc):
    picked = jnp.take(returned, flat_pos, axis=0)
    return jnp.sum(gate_loc[:, :, None] * picked.astype(jnp.float32), axis=1).astype(jnp.bfloat16)


def expert_ffn(rows_in, wg_loc, wu_loc, wd_loc):
    pre_gate = jnp.einsum("erd,edf->erf", rows_in, wg_loc, preferred_element_type=jnp.float32)
    pre_up = jnp.einsum("erd,edf->erf", rows_in, wu_loc, preferred_element_type=jnp.float32)
    hidden = (jax.nn.silu(pre_gate) * pre_up).astype(jnp.bfloat16)
    return jnp.einsum("erf,efd->erd", hidden, wd_loc, preferred_element_type=jnp.float32).astype(jnp.bfloat16)


def solution(mesh):
    group_n = mesh.shape["ep"]
    row_spec = P(("dp", "ep"))
    expert_spec = P("ep")

    def local_step(tok_loc, route_loc, gate_loc, wg_loc, wu_loc, wd_loc):
        local_n = wg_loc.shape[0]
        tok_dev, d_model = tok_loc.shape
        capacity = tok_dev // 2
        row_ids, slot_pos = pack_index(route_loc, local_n * group_n, capacity)
        row_ids = row_ids.reshape(group_n, local_n, capacity).transpose(1, 0, 2)
        send_buf = jnp.take(tok_loc, row_ids, axis=0, mode="fill", fill_value=0)
        recv_buf = lax.all_to_all(send_buf, "ep", 1, 1, tiled=True)
        expert_out = expert_ffn(recv_buf.reshape(local_n, group_n * capacity, d_model), wg_loc, wu_loc, wd_loc)
        returned = lax.all_to_all(expert_out.reshape(local_n, group_n, capacity, d_model), "ep", 1, 1, tiled=True)
        flat_pos = ((route_loc % local_n) * group_n + route_loc // local_n) * capacity + slot_pos
        return combine_rows(returned.reshape(-1, d_model), flat_pos, gate_loc)

    return jax.shard_map(local_step, mesh=mesh, in_specs=(row_spec, row_spec, row_spec, expert_spec, expert_spec, expert_spec), out_specs=row_spec, check_vma=False)
```

profile of v0, /device:TPU:112, one launch (start us, length us, event | category | flops | bytes accessed | tf_op | source)
XLA Modules:
  0.0 406.2 jit_solution(6398625639585955954)
XLA Ops:
  0.0 0.8 copy.56
  0.8 0.2 convert_reduce_fusion
  1.2 0.5 copy-done.2
  1.7 97.1 %while.24 = (s32[]{:T(128)}, u32[64,32]{1,0:T(8,128)S(1)}, u32[64,32]{1,0:T(8,128)S(1)}, s32[64,64]{1,0:T(8,128)S(1)}, s32[]{:T(128)}, /*index=5*/s32[]{:T(128)}) while((s32[]{:T(128)}, u32[64,32]{1,0:T(8,128)S(1)}, u32[64,32]{1,0:T(8,128)S(1)}, s32[64,64]{1,0:T(8,128)S(1)}, s32[]{:T(128)}, /*index=5*/s32[]{:T(128)}) %tuple.39), condition=%wide.region_3.4_spmd.clone, body=%wide.region_2.3_spmd.clone.sunk | while | flops 47139 | bytes 168273 | solution.py:12
  1.8 13.6 %gather_fusion = s32[2048]{0:T(1024)S(1)} fusion(s32[64,64]{1,0:T(8,128)S(1)} %get-tuple-element.164, u32[2048]{0:T(1024)S(1)} %reshape.93), kind=kCustom, calls=%fused_computation.clone.clone.1 | custom fusion | bytes 32768 | tf_op jit(solution)/shard_map/vmap(jit(searchsorted))/vmap(jit(_searchsorted_scan_impl))/while/body/eval_jaxpr/gather | solution.py:12
  15.7 13.6 %gather_fusion = s32[2048]{0:T(1024)S(1)} fusion(s32[64,64]{1,0:T(8,128)S(1)} %get-tuple-element.164, u32[2048]{0:T(1024)S(1)} %reshape.93), kind=kCustom, calls=%fused_computation.clone.clone.1 | custom fusion | bytes 32768 | tf_op jit(solution)/shard_map/vmap(jit(searchsorted))/vmap(jit(_searchsorted_scan_impl))/while/body/eval_jaxpr/gather | solution.py:12
  29.5 13.6 %gather_fusion = s32[2048]{0:T(1024)S(1)} fusion(s32[64,64]{1,0:T(8,128)S(1)} %get-tuple-element.164, u32[2048]{0:T(1024)S(1)} %reshape.93), kind=kCustom, calls=%fused_computation.clone.clone.1 | custom fusion | bytes 32768 | tf_op jit(solution)/shard_map/vmap(jit(searchsorted))/vmap(jit(_searchsorted_scan_impl))/while/body/eval_jaxpr/gather | solution.py:12
  43.4 13.6 %gather_fusion = s32[2048]{0:T(1024)S(1)} fusion(s32[64,64]{1,0:T(8,128)S(1)} %get-tuple-element.164, u32[2048]{0:T(1024)S(1)} %reshape.93), kind=kCustom, calls=%fused_computation.clone.clone.1 | custom fusion | bytes 32768 | tf_op jit(solution)/shard_map/vmap(jit(searchsorted))/vmap(jit(_searchsorted_scan_impl))/while/body/eval_jaxpr/gather | solution.py:12
  57.3 13.6 %gather_fusion = s32[2048]{0:T(1024)S(1)} fusion(s32[64,64]{1,0:T(8,128)S(1)} %get-tuple-element.164, u32[2048]{0:T(1024)S(1)} %reshape.93), kind=kCustom, calls=%fused_computation.clone.clone.1 | custom fusion | bytes 32768 | tf_op jit(solution)/shard_map/vmap(jit(searchsorted))/vmap(jit(_searchsorted_scan_impl))/while/body/eval_jaxpr/gather | solution.py:12
  71.2 13.6 %gather_fusion = s32[2048]{0:T(1024)S(1)} fusion(s32[64,64]{1,0:T(8,128)S(1)} %get-tuple-element.164, u32[2048]{0:T(1024)S(1)} %reshape.93), kind=kCustom, calls=%fused_computation.clone.clone.1 | custom fusion | bytes 32768 | tf_op jit(solution)/shard_map/vmap(jit(searchsorted))/vmap(jit(_searchsorted_scan_impl))/while/body/eval_jaxpr/gather | solution.py:12
  85.0 13.6 %gather_fusion = s32[2048]{0:T(1024)S(1)} fusion(s32[64,64]{1,0:T(8,128)S(1)} %get-tuple-element.164, u32[2048]{0:T(1024)S(1)} %reshape.93), kind=kCustom, calls=%fused_computation.clone.clone.1 | custom fusion | bytes 32768 | tf_op jit(solution)/shard_map/vmap(jit(searchsorted))/vmap(jit(_searchsorted_scan_impl))/while/body/eval_jaxpr/gather | solution.py:12
  99.0 11.0 %gather_fusion.1 = bf16[2048,2048]{1,0:T(8,128)(2,1)} fusion(bf16[64,2048]{1,0:T(8,128)(2,1)S(1)} %copy-done, s32[2048]{0:T(1024)S(1)} %broadcast_clamp_fusion), kind=kCustom, calls=%fused_computation.1 | custom fusion | bytes 16785408 | tf_op jit(solution)/shard_map/jit(_take)/gather | solution.py:40
  109.9 4.4 %copy_select_fusion = bf16[8,8,32,2048]{3,2,0,1:T(8,128)(2,1)S(1)} fusion(bf16[8,8,32,2048]{3,2,1,0:T(8,128)(2,1)} %bitcast.32, pred[8,8,32]{2,0,1:T(8,128)(4,1)S(1)} %copy.62), kind=kLoop, calls=%fused_computation.11 | loop fusion | flops 4194304 | bytes 16779264 | tf_op jit(solution)/shard_map/jit(_take)/select_n | solution.py:40
  114.3 99.8 %all_to_all.10 = bf16[8,8,32,2048]{3,2,0,1:T(8,128)(2,1)} all-to-all(bf16[8,8,32,2048]{3,2,0,1:T(8,128)(2,1)S(1)} %copy_select_fusion), channel_id=1, replica_groups=mesh['dp'=2,'ep'=8] {'ep'}, dimensions={1} | all-to-all | bytes 16777216 | tf_op jit(solution)/shard_map/all_to_all | solution.py:41
  214.1 8.3 %copy.64 = bf16[8,8,32,2048]{3,2,1,0:T(8,128)(2,1)} copy(bf16[8,8,32,2048]{3,2,0,1:T(8,128)(2,1)} %all_to_all.10) | data formatting | bytes 16777216 | tf_op jit(solution)/shard_map/all_to_all | solution.py:41
  222.4 22.8 %fusion.14 = f32[8,256,1024]{2,1,0:T(8,128)} fusion(bf16[8,256,2048]{2,1,0:T(8,128)(2,1)} %bitcast.33, bf16[8,2048,1024]{2,1,0:T(8,128)(2,1)} %param.11), kind=kOutput, calls=%fused_computation.44 | convolution fusion | flops 8589934592 | bytes 50331648 | tf_op jit(solution)/shard_map/erd,edf->erf/dot_general | solution.py:23
  245.2 32.7 %convolution_convert_fusion = bf16[8,256,2048]{2,1,0:T(8,128)(2,1)} fusion(bf16[8,1024,2048]{2,1,0:T(8,128)(2,1)} %param.13, f32[8,256,1024]{2,1,0:T(8,128)} %fusion.14, bf16[8,256,2048]{2,1,0:T(8,128)(2,1)} %bitcast.34, bf16[8,2048,1024]{2,1,0:T(8,128)(2,1)} %param.12), kind=kOutput, calls=%fused_computation.13 | convolution fusion | flops 17196646400 | bytes 92274688 | tf_op jit(solution)/shard_map/erf,efd->erd/dot_general | solution.py:26
  277.9 8.3 %copy.65 = bf16[8,8,32,2048]{3,2,0,1:T(8,128)(2,1)} copy(bf16[8,8,32,2048]{3,2,1,0:T(8,128)(2,1)} %bitcast.35) | data formatting | bytes 16777216 | tf_op jit(solution)/shard_map/reshape | solution.py:43
  286.2 5.4 %all-to-all-start.1 = ((bf16[8,8,32,2048]{3,2,0,1:T(8,128)(2,1)}), bf16[8,8,32,2048]{3,2,0,1:T(8,128)(2,1)}, u32[]{:S(2)}, u32[]{:S(2)}) async-start(bf16[8,8,32,2048]{3,2,0,1:T(8,128)(2,1)} %copy.65), calls=%async_computation.1 | async-start | bytes 16777216 | tf_op jit(solution)/shard_map/all_to_all | solution.py:43
  291.9 3.8 gather_fusion.3
  296.2 89.6 %all-to-all-done.1 = bf16[8,8,32,2048]{3,2,0,1:T(8,128)(2,1)} async-done(((bf16[8,8,32,2048]{3,2,0,1:T(8,128)(2,1)}), bf16[8,8,32,2048]{3,2,0,1:T(8,128)(2,1)}, u32[]{:S(2)}, u32[]{:S(2)}) %all-to-all-start.1) | async-done | bytes 8388640 | tf_op jit(solution)/shard_map/all_to_all | solution.py:43
  385.8 8.3 %copy.66 = bf16[8,8,32,2048]{3,2,1,0:T(8,128)(2,1)} copy(bf16[8,8,32,2048]{3,2,0,1:T(8,128)(2,1)} %all-to-all-done.1) | data formatting | bytes 16777216 | tf_op jit(solution)/shard_map/all_to_all | solution.py:43
  394.1 8.9 %gather_fusion.2 = bf16[512,2048]{1,0:T(8,128)(2,1)S(1)} fusion(bf16[2048,2048]{1,0:T(8,128)(2,1)} %bitcast.31, s32[1024]{0:T(1024)S(1)} %pad_clamp_fusion), kind=kCustom, calls=%fused_computation.2 | custom fusion | bytes 4196352 | tf_op jit(solution)/shard_map/jit(_take)/gather | solution.py:18
  403.0 3.2 multiply_reduce_fusion
  (81 shorter events, 2.5 us)
Async XLA Ops:
  0.0 99.0 %copy-start = (bf16[64,2048]{1,0:T(8,128)(2,1)S(1)}, bf16[64,2048]{1,0:T(8,128)(2,1)}, u32[]{:S(2)}) copy-start(bf16[64,2048]{1,0:T(8,128)(2,1)} %param.8) | copy-start | bytes 786436
  1.1 0.6 copy-start.2
  286.2 5.5 %copy-start.4 = (s32[64,8]{0,1:T(8,128)S(1)}, s32[64,8]{0,1:T(8,128)}, u32[]{:S(2)}) copy-start(s32[64,8]{0,1:T(8,128)} %param.9) | copy-start | bytes 6148
  286.2 5.7 %copy-start.3 = (s32[64,64]{1,0:T(8,128)S(1)}, s32[64,64]{1,0:T(8,128)}, u32[]{:S(2)}) copy-start(s32[64,64]{1,0:T(8,128)} %copy-done.2) | copy-start | bytes 49156
  286.2 99.6 %all-to-all-start.1 = ((bf16[8,8,32,2048]{3,2,0,1:T(8,128)(2,1)}), bf16[8,8,32,2048]{3,2,0,1:T(8,128)(2,1)}, u32[]{:S(2)}, u32[]{:S(2)}) async-start(bf16[8,8,32,2048]{3,2,0,1:T(8,128)(2,1)} %copy.65), calls=%async_computation.1 | async-start | bytes 16777216 | tf_op jit(solution)/shard_map/all_to_all | solution.py:43
  291.9 4.3 %copy-start.5 = (f32[64,8]{0,1:T(8,128)S(1)}, f32[64,8]{0,1:T(8,128)}, u32[]{:S(2)}) copy-start(f32[64,8]{0,1:T(8,128)} %param.10) | copy-start | bytes 6148
  394.1 12.1 %copy-start.1 = (bf16[64,2048]{1,0:T(8,128)(2,1)S(1)}, bf16[64,2048]{1,0:T(8,128)(2,1)}, u32[]{:S(2)}) copy-start(bf16[64,2048]{1,0:T(8,128)(2,1)} %param.8) | copy-start | bytes 786436
where the time goes:
time: 407 us; the launch traced here: 406 us
  local copies, waits for them, and re-layouts  147 us (36%)
  blocking collectives  99.8 us (25%)
  waiting for transfers between devices  89.6 us (22%)
  matrix products  55.5 us (14%)
  other arithmetic  8.35 us (2%)
  starting transfers between devices  5.44 us (1%)
    all_to_all x1, blocking collectives, local_step(): recv_buf = lax.all_to_all(send_buf, 'ep', 1, 1, tiled=True)  99.8 us
    gather x14, local copies, waits for them, and re-layouts, pack_index(): jnp.searchsorted(column, targets, side='left')  95.8 us
    all_to_all x1, waiting for transfers between devices, local_step(): lax.all_to_all(expert_out.reshape(local_n, group_n, capacity, d_model), '...  89.6 us
    dot_general x1, matrix products, expert_ffn(): jnp.einsum('erf,efd->erd', hidden, wd_loc, preferred_element_type=jnp.flo...  32.7 us
    dot_general x1, matrix products, expert_ffn(): jnp.einsum('erd,edf->erf', rows_in, wg_loc, preferred_element_type=jnp.fl...  22.8 us
    gather x1, local copies, waits for them, and re-layouts, local_step(): send_buf = jnp.take(tok_loc, row_ids, axis=0, mode='fill', fill_value=0)  11 us
    gather x1, local copies, waits for them, and re-layouts, combine_rows(): picked = jnp.take(returned, flat_pos, axis=0)  8.91 us
    all_to_all x1, local copies, waits for them, and re-layouts, local_step(): lax.all_to_all(expert_out.reshape(local_n, group_n, capacity, d_model), '...  8.27 us
  transfers between devices with their start and end apart: 1, of which 1 were waited for; matrix products, arithmetic and copies ran while one was open for 1% of the time, Pallas kernels for 0%

commit v1 on v0

v1 whole, which is shorter than its diff:
```python
import functools

import jax
import jax.numpy as jnp
from jax import lax
from jax.experimental import pallas as pl
from jax.experimental.pallas import tpu as pltpu
from jax.sharding import PartitionSpec as P

F32 = jnp.float32
BF16 = jnp.bfloat16
KCHUNKS = 4
COLS = 256
WSLOTS = 8
DSLOTS = 2


def moe_kernel(dims, x_hbm, comb_in, wg_hbm, wu_hbm, wd_hbm, y_ref,
               xbuf, comb, codes, pmat, smat, gmat, gacc, uacc, hid, wgb, wub, wdb, acc, sib, red, ra, rb, rl, rr,
               x_sem, comb_send, comb_recv, ag_send, ag_recv, w_sem, d_sem, rs_send, rs_recv):
    n, tok_dev, d_model, d_ff, n_exp, top_k, cap = dims
    chips = n // 2
    kw = d_model // KCHUNKS
    n_items = KCHUNKS * n_exp
    n_chunks = d_model // COLS
    half_tok = n * tok_dev // 2
    half_slot = n * cap // 2

    me = lax.axis_index("ep")
    chip, core = me // 2, me % 2
    sibling = chip * 2 + (1 - core)
    c_right, c_left, c_opp = (chip + 1) % chips, (chip + chips - 1) % chips, (chip + 2) % chips
    right, left, opp = c_right * 2 + core, c_left * 2 + core, c_opp * 2 + core
    other = 1 - core

    def remote(src, dst, send, recv, dev):
        return pltpu.make_async_remote_copy(src_ref=src, dst_ref=dst, send_sem=send, recv_sem=recv,
                                            device_id={"ep": dev}, device_id_type=pl.DeviceIdType.MESH)

    def x_copy(kc):
        return pltpu.make_async_copy(x_hbm.at[:, pl.ds(kc * kw, kw)],
                                     xbuf.at[kc, pl.ds(pl.multiple_of(me * tok_dev, tok_dev), tok_dev), :], x_sem.at[kc])

    def w_copies(item):
        e, kc, slot = item % n_exp, item // n_exp, item % WSLOTS
        rows = pl.ds(pl.multiple_of(kc * kw, kw), kw)
        return (pltpu.make_async_copy(wg_hbm.at[e, rows, :], wgb.at[slot], w_sem.at[slot, 0]),
                pltpu.make_async_copy(wu_hbm.at[e, rows, :], wub.at[slot], w_sem.at[slot, 1]))

    def d_copy(c):
        slot = c % DSLOTS
        return pltpu.make_async_copy(wd_hbm.at[:, :, pl.ds(pl.multiple_of(c * COLS, COLS), COLS)], wdb.at[slot], d_sem.at[slot])

    for kc in range(KCHUNKS):
        x_copy(kc).start()
    for item in range(WSLOTS):
        for copy in w_copies(item):
            copy.start()

    barrier = pltpu.get_barrier_semaphore()
    for off in range(1, n):
        pl.semaphore_signal(barrier, inc=1, device_id={"ep": (me + off) % n}, device_id_type=pl.DeviceIdType.MESH)
    pl.semaphore_wait(barrier, n - 1)

    def block(kc, src):
        return xbuf.at[kc, pl.ds(pl.multiple_of(src * tok_dev, tok_dev), tok_dev), :]

    def ag_copy(kc, src, lane, dev):
        return remote(block(kc, src), block(kc, src), ag_send.at[kc, lane], ag_recv.at[kc, src], dev)

    def send_own(kc):
        x_copy(kc).wait()
        ag_copy(kc, me, 0, right).start()
        ag_copy(kc, me, 1, left).start()
        ag_copy(kc, me, 2, sibling).start()

    def relay_near(kc):
        ag_copy(kc, left, 3, sibling).wait_recv()
        ag_copy(kc, right, 4, sibling).wait_recv()
        if kc % 2 == 0:
            ag_copy(kc, left, 5, right).start()
        else:
            ag_copy(kc, right, 5, left).start()
        ag_copy(kc, left, 3, sibling).start()
        ag_copy(kc, right, 4, sibling).start()

    def relay_far(kc):
        ag_copy(kc, opp, 6, sibling).wait_recv()
        ag_copy(kc, opp, 6, sibling).start()

    def gathered(kc):
        for c in (chip, c_left, c_right, c_opp):
            ag_copy(kc, c * 2 + other, 2, sibling).wait_recv()

    send_own(0)
    comb_copies = []
    for off in range(1, n):
        copy = remote(comb_in, comb.at[me], comb_send.at[off - 1], comb_recv.at[me], (me + off) % n)
        copy.start()
        comb_copies.append(copy)
    comb[me] = comb_in[...]
    send_own(1)

    acc[...] = jnp.zeros_like(acc)

    for off in range(1, n):
        src = (me + off) % n
        remote(comb_in, comb.at[src], comb_send.at[off - 1], comb_recv.at[src], src).wait_recv()

    lanes = 2 * tok_dev
    t_row = lax.broadcasted_iota(jnp.int32, (lanes, lanes), 0)
    t_col = lax.broadcasted_iota(jnp.int32, (lanes, lanes), 1)
    before = jnp.where((t_row < t_col) & (t_row // tok_dev == t_col // tok_dev), 1.0, 0.0).astype(BF16)
    e_id = (lax.broadcasted_iota(jnp.int32, (n_exp, lanes), 0) + me * n_exp).astype(F32)
    lane_base = ((lax.broadcasted_iota(jnp.int32, (n_exp, lanes), 1) // tok_dev) * cap).astype(F32)
    for c in range(chips):
        both = comb[2 * c] + comb[2 * c + 1]
        hits = jnp.zeros((n_exp, lanes), F32)
        gates = jnp.zeros((n_exp, lanes), F32)
        for k in range(top_k):
            same = jnp.broadcast_to(both[k:k + 1, :], (n_exp, lanes)) == e_id
            hits = hits + jnp.where(same, 1.0, 0.0)
            gates = gates + jnp.where(same, jnp.broadcast_to(both[top_k + k:top_k + k + 1, :], (n_exp, lanes)), 0.0)
        rank = jnp.dot(hits.astype(BF16), before, preferred_element_type=F32)
        code = jnp.where(hits > 0.0, rank + lane_base + float((c % 2) * 2 * cap), -1.0)
        codes[c, 0:n_exp, :] = code
        codes[c, n_exp:2 * n_exp, :] = gates

    def tables(e, carry):
        slot_row = lax.broadcasted_iota(jnp.int32, (half_slot, lanes), 0).astype(F32)
        slot_col = lax.broadcasted_iota(jnp.int32, (lanes, half_slot), 1).astype(F32)
        for c in range(chips):
            code = jnp.broadcast_to(codes[c, pl.ds(e, 1), :], (half_slot, lanes))
            pmat[e, c // 2, :, (c % 2) * lanes:(c % 2 + 1) * lanes] = jnp.where(code == slot_row, 1.0, 0.0).astype(BF16)
            smat[e, c // 2, (c % 2) * lanes:(c % 2 + 1) * lanes, :] = jnp.where(code.T == slot_col, 1.0, 0.0).astype(BF16)
            gate = jnp.broadcast_to(codes[c, pl.ds(n_exp + e, 1), :], (lanes, lanes))
            gmat[e, c * lanes:(c + 1) * lanes, :] = gate.T
        return carry

    relay_near(0)
    send_own(2)
    lax.fori_loop(0, n_exp, tables, 0)
    relay_far(0)
    gathered(0)

    def expert_chunk(kc, e):
        item = kc * n_exp + e
        slot = item % WSLOTS
        for copy in w_copies(item):
            copy.wait()
        rows = [jnp.dot(pmat[e, h], xbuf[kc, h * half_tok:(h + 1) * half_tok, :], preferred_element_type=F32) for h in range(2)]
        xs = jnp.concatenate(rows, axis=0).astype(BF16)
        for c in range(d_ff // 256):
            cols = slice(c * 256, (c + 1) * 256)
            g = jnp.dot(xs, wgb[slot, :, cols], preferred_element_type=F32)
            u = jnp.dot(xs, wub[slot, :, cols], preferred_element_type=F32)
            if kc > 0:
                g = gacc[e, :, cols] + g
                u = uacc[e, :, cols] + u
            if kc < KCHUNKS - 1:
                gacc[e, :, cols] = g
                uacc[e, :, cols] = u
            else:
                hid[e, :, cols] = (jax.nn.silu(g) * u).astype(BF16)

        @pl.when(item + WSLOTS < n_items)
        def _():
            for copy in w_copies(item + WSLOTS):
                copy.start()

    for kc in range(KCHUNKS):
        def body(e, carry, kc=kc):
            expert_chunk(kc, e)
            nxt = kc + 1
            if nxt < KCHUNKS:
                @pl.when(e == 1)
                def _():
                    relay_near(nxt)
                    if nxt + 2 < KCHUNKS:
                        send_own(nxt + 2)

                @pl.when(e == n_exp - 3)
                def _():
                    relay_far(nxt)
            else:
                @pl.when(e < DSLOTS)
                def _():
                    d_copy(e).start()
            return carry

        lax.fori_loop(0, n_exp, body, 0)
        if kc + 1 < KCHUNKS:
            gathered(kc + 1)

    def to_sibling(c):
        return remote(acc.at[c, :, other], sib.at[c], rs_send.at[0, c], rs_recv.at[0, c], sibling)

    def far_right(c):
        return remote(red.at[c, c_opp, :, pl.ds(0, COLS // 2)], ra.at[c], rs_send.at[1, c], rs_recv.at[1, c], right)

    def far_left(c):
        return remote(red.at[c, c_opp, :, pl.ds(COLS // 2, COLS // 2)], rb.at[c], rs_send.at[2, c], rs_recv.at[2, c], left)

    def near_right(c):
        return remote(red.at[c, c_right], rl.at[c], rs_send.at[3, c], rs_recv.at[3, c], right)

    def near_left(c):
        return remote(red.at[c, c_left], rr.at[c], rs_send.at[4, c], rs_recv.at[4, c], left)

    def stage2(c):
        to_sibling(c).wait_recv()
        red[c] = acc[c, :, core] + sib[c]
        far_right(c).start()
        far_left(c).start()

    def stage3(c):
        far_right(c).wait_recv()
        red[c, c_right, :, :COLS // 2] = red[c, c_right, :, :COLS // 2] + ra[c]
        near_right(c).start()
        far_left(c).wait_recv()
        red[c, c_left, :, COLS // 2:] = red[c, c_left, :, COLS // 2:] + rb[c]
        near_left(c).start()

    def stage4(c):
        near_right(c).wait_recv()
        near_left(c).wait_recv()
        y_ref[:, pl.ds(pl.multiple_of(c * COLS, COLS), COLS)] = (red[c, chip] + rl[c] + rr[c]).astype(BF16)

    def down(c):
        slot = c % DSLOTS
        d_copy(c).wait()
        for e in range(n_exp):
            out = jnp.dot(hid[e], wdb[slot, e], preferred_element_type=F32).astype(BF16)
            for ch in range(chips):
                h, rows = ch // 2, slice((ch % 2) * lanes, (ch % 2 + 1) * lanes)
                put = jnp.dot(smat[e, h, rows, :], out[h * half_slot:(h + 1) * half_slot], preferred_element_type=F32)
                gate = gmat[e, ch * lanes:(ch + 1) * lanes, :]
                put = put * jnp.concatenate([gate] * (COLS // lanes), axis=1)
                acc[c, ch] = acc[c, ch] + put.reshape(2, tok_dev, COLS)

        @pl.when(c + DSLOTS < n_chunks)
        def _():
            d_copy(c + DSLOTS).start()

    def chunk_body(c, carry):
        down(c)
        to_sibling(c).start()

        @pl.when(c >= 1)
        def _():
            stage2(c - 1)

        @pl.when(c >= 2)
        def _():
            stage3(c - 2)

        @pl.when(c >= 3)
        def _():
            stage4(c - 3)
        return carry

    lax.fori_loop(0, n_chunks, chunk_body, 0)
    last = n_chunks - 1
    stage2(last)
    stage3(last - 1)
    stage4(last - 2)
    stage3(last)
    stage4(last - 1)
    stage4(last)

    for copy in comb_copies:
        copy.wait_send()
    for kc in range(KCHUNKS):
        for lane, (src, dev) in enumerate(((me, right), (me, left), (me, sibling), (left, sibling), (right, sibling),
                                           (left, right) if kc % 2 == 0 else (right, left), (opp, sibling))):
            ag_copy(kc, src, lane, dev).wait_send()

    def drain(c, carry):
        for make in (to_sibling, far_right, far_left, near_right, near_left):
            make(c).wait_send()
        return carry

    lax.fori_loop(0, n_chunks, drain, 0)


def solution(mesh):
    n = mesh.shape["ep"]
    row_spec = P(("dp", "ep"))
    expert_spec = P("ep")

    def local_step(tok, route, gate, wg, wu, wd):
        tok_dev, d_model = tok.shape
        n_exp, _, d_ff = wg.shape
        top_k = route.shape[1]
        cap = tok_dev // 2
        chips = n // 2
        lanes = 2 * tok_dev
        kw = d_model // KCHUNKS
        n_chunks = d_model // COLS
        dims = (n, tok_dev, d_model, d_ff, n_exp, top_k, cap)

        table = jnp.concatenate([route.astype(F32).T, gate.T], axis=0)
        mine = lax.broadcasted_iota(jnp.int32, (1, lanes), 1) // tok_dev == lax.axis_index("ep") % 2
        empty = jnp.where(lax.broadcasted_iota(jnp.int32, (2 * top_k, 1), 0) < top_k, 0.0, 0.0)
        table = jnp.where(mine, jnp.concatenate([table, table], axis=1), empty)

        hbm = pl.BlockSpec(memory_space=pl.ANY)
        vmem = pl.BlockSpec(memory_space=pltpu.VMEM)
        return pl.pallas_call(
            functools.partial(moe_kernel, dims),
            out_shape=jax.ShapeDtypeStruct((tok_dev, d_model), BF16),
            in_specs=[hbm, vmem, hbm, hbm, hbm],
            out_specs=vmem,
            scratch_shapes=[
                pltpu.VMEM((KCHUNKS, n * tok_dev, kw), BF16),
                pltpu.VMEM((n, 2 * top_k, lanes), F32),
                pltpu.VMEM((chips, 2 * n_exp, lanes), F32),
                pltpu.VMEM((n_exp, 2, n * cap // 2, n * tok_dev // 2), BF16),
                pltpu.VMEM((n_exp, 2, n * tok_dev // 2, n * cap // 2), BF16),
                pltpu.VMEM((n_exp, n * tok_dev, lanes), F32),
                pltpu.VMEM((n_exp, n * cap, d_ff), F32),
                pltpu.VMEM((n_exp, n * cap, d_ff), F32),
                pltpu.VMEM((n_exp, n * cap, d_ff), BF16),
                pltpu.VMEM((WSLOTS, kw, d_ff), BF16),
                pltpu.VMEM((WSLOTS, kw, d_ff), BF16),
                pltpu.VMEM((DSLOTS, n_exp, d_ff, COLS), BF16),
                pltpu.VMEM((n_chunks, chips, 2, tok_dev, COLS), F32),
                pltpu.VMEM((n_chunks, chips, tok_dev, COLS), F32),
                pltpu.VMEM((n_chunks, chips, tok_dev, COLS), F32),
                pltpu.VMEM((n_chunks, tok_dev, COLS // 2), F32),
                pltpu.VMEM((n_chunks, tok_dev, COLS // 2), F32),
                pltpu.VMEM((n_chunks, tok_dev, COLS), F32),
                pltpu.VMEM((n_chunks, tok_dev, COLS), F32),
                pltpu.SemaphoreType.DMA((KCHUNKS,)),
                pltpu.SemaphoreType.DMA((n - 1,)),
                pltpu.SemaphoreType.DMA((n,)),
                pltpu.SemaphoreType.DMA((KCHUNKS, 7)),
                pltpu.SemaphoreType.DMA((KCHUNKS, n)),
                pltpu.SemaphoreType.DMA((WSLOTS, 2)),
                pltpu.SemaphoreType.DMA((DSLOTS,)),
                pltpu.SemaphoreType.DMA((5, n_chunks)),
                pltpu.SemaphoreType.DMA((5, n_chunks)),
            ],
            compiler_params=pltpu.CompilerParams(collective_id=0, has_side_effects=True, vmem_limit_bytes=67_043_328),
        )(tok, table, wg, wu, wd)

    return jax.shard_map(local_step, mesh=mesh, in_specs=(row_spec, row_spec, row_spec, expert_spec, expert_spec, expert_spec), out_specs=row_spec, check_vma=False)
```

time: 407 us -> 93.3 us (0.23)
  local copies, waits for them, and re-layouts: 147 us -> 1.67 us
  blocking collectives: 99.8 us -> 0 us
  waiting for transfers between devices: 89.6 us -> 0 us
  Pallas kernels: 0 us -> 89.3 us
  matrix products: 55.5 us -> 0 us
  other arithmetic: 8.35 us -> 2.13 us
  starting transfers between devices: 5.44 us -> 0 us
    gather x21 -> x0, local copies, waits for them, and re-layouts: 120 us -> none  [the longest x14 95.8 us: pack_index(): jnp.searchsorted(column, targets, side='left')]
    all_to_all x1 -> x0, blocking collectives: 99.8 us -> none  [local_step(): recv_buf = lax.all_to_all(send_buf, 'ep', 1, 1, tiled=True)]
    all_to_all x1 -> x0, waiting for transfers between devices: 89.6 us -> none  [local_step(): lax.all_to_all(expert_out.reshape(local_n, group_n, capacity, d_model), '...]
    pallas_call x0 -> x1, Pallas kernels: none -> 89.3 us  [local_step(): pl.pallas_call(functools.partial(moe_kernel, dims), out_shape=jax.ShapeDt...]
    dot_general x2 -> x0, matrix products: 55.5 us -> none  [the longest x1 32.7 us: expert_ffn(): jnp.einsum('erf,efd->erd', hidden, wd_loc, preferred_element_type=jnp.flo...]
    all_to_all x2 -> x0, local copies, waits for them, and re-layouts: 16.5 us -> none  [the longest x1 8.27 us: local_step(): lax.all_to_all(expert_out.reshape(local_n, group_n, capacity, d_model), '...]
    reshape x1 -> x0, local copies, waits for them, and re-layouts: 8.27 us -> none  [local_step(): expert_out.reshape(local_n, group_n, capacity, d_model)]
    all_to_all x1 -> x0, starting transfers between devices: 5.44 us -> none  [local_step(): lax.all_to_all(expert_out.reshape(local_n, group_n, capacity, d_model), '...]
  transfers between devices with their start and end apart: 1 -> 0, of which waited for: 1 -> 0; matrix products, arithmetic and copies ran while one was open for 1% -> 0% of each run, Pallas kernels for 0% -> 0%
where the time goes in v1:
time: 93.3 us; the launch traced here: 93.1 us
  Pallas kernels  89.3 us (96%)
  other arithmetic  2.13 us (2%)
  local copies, waits for them, and re-layouts  1.67 us (2%)
    pallas_call x1, Pallas kernels, local_step(): pl.pallas_call(functools.partial(moe_kernel, dims), out_shape=jax.ShapeDt...  89.3 us

profile of v1, /device:TPU:112, one launch (start us, length us, event | category | flops | bytes accessed | tf_op | source)
XLA Modules:
  0.0 93.1 jit_solution(18257899099284405139)
XLA Ops:
  0.0 0.7 convert_bitcast_fusion
  0.7 1.4 %maximum_select_fusion.comb_in = f32[16,128]{1,0:T(8,128)} fusion(f32[8,64]{1,0:T(8,128)} %bitcast.3, f32[8,64]{1,0:T(8,128)S(1)} %convert_bitcast_fusion, pred[128]{0:T(512)(128)(4,1)S(1)} %fusion), kind=kLoop, calls=%fused_computation | loop fusion | flops 8192 | bytes 12416 | tf_op jit(solution)/shard_map/jit(_where)/select_n | solution.py:305
  2.1 89.3 %shard_map.64 = bf16[64,2048]{1,0:T(8,128)(2,1)} custom-call(bf16[64,2048]{1,0:T(8,128)(2,1)} %x_hbm.1, f32[16,128]{1,0:T(8,128)} %maximum_select_fusion.comb_in, bf16[8,2048,1024]{2,1,0:T(8,128)(2,1)} %wg_hbm.1, bf16[8,2048,1024]{2,1,0:T(8,128)(2,1)} %wu_hbm.1, bf16[8,1024,2048]{2,1,0:T(8,128)(2,1)} %wd_hbm.1), custom_call_target="tpu_custom_call" | custom-call | tf_op jit(solution)/shard_map/pallas_call | solution.py:309
  91.4 1.7 %copy.8 = bf16[64,2048]{1,0:T(8,128)(2,1)} copy(bf16[64,2048]{1,0:T(8,128)(2,1)} %shard_map.64) | data formatting | bytes 524288
  (1 shorter events, 0.0 us)

commit v2 on v1

--- a/solution.py
+++ b/solution.py
@@ -11,17 +11,18 @@
 BF16 = jnp.bfloat16
 KCHUNKS = 4
 COLS = 256
-WSLOTS = 8
-DSLOTS = 2
-
-
-def moe_kernel(dims, x_hbm, comb_in, wg_hbm, wu_hbm, wd_hbm, y_ref,
-               xbuf, comb, codes, pmat, smat, gmat, gacc, uacc, hid, wgb, wub, wdb, acc, sib, red, ra, rb, rl, rr,
-               x_sem, comb_send, comb_recv, ag_send, ag_recv, w_sem, d_sem, rs_send, rs_recv):
+SLOTS = 26
+
+
+def moe_kernel(dims, x_hbm, route_ref, gate_ref, wg_hbm, wu_hbm, wd_hbm, y_ref,
+               xbuf, table, comb_in, comb, codes, pmat, smat, gmat, gacc, uacc, hid, ring, outs, acc, sib, ra, rb, rl, rr,
+               x_sem, comb_send, comb_recv, ag_send, ag_recv, w_sem, rs_send, rs_recv):
     n, tok_dev, d_model, d_ff, n_exp, top_k, cap = dims
     chips = n // 2
     kw = d_model // KCHUNKS
-    n_items = KCHUNKS * n_exp
+    n_gate = 2 * KCHUNKS * n_exp
+    wide = d_ff // 2
+    n_items = n_gate + n_exp * (d_model // wide)
     n_chunks = d_model // COLS
     half_tok = n * tok_dev // 2
     half_slot = n * cap // 2
@@ -41,21 +42,34 @@
         return pltpu.make_async_copy(x_hbm.at[:, pl.ds(kc * kw, kw)],
                                      xbuf.at[kc, pl.ds(pl.multiple_of(me * tok_dev, tok_dev), tok_dev), :], x_sem.at[kc])
 
-    def w_copies(item):
-        e, kc, slot = item % n_exp, item // n_exp, item % WSLOTS
+    def ring_copy(src, slot, j):
+        return pltpu.make_async_copy(src, ring.at[slot, pl.ds(j * kw, kw), :], w_sem.at[slot, j])
+
+    def start_gate(kc, e, item):
         rows = pl.ds(pl.multiple_of(kc * kw, kw), kw)
-        return (pltpu.make_async_copy(wg_hbm.at[e, rows, :], wgb.at[slot], w_sem.at[slot, 0]),
-                pltpu.make_async_copy(wu_hbm.at[e, rows, :], wub.at[slot], w_sem.at[slot, 1]))
-
-    def d_copy(c):
-        slot = c % DSLOTS
-        return pltpu.make_async_copy(wd_hbm.at[:, :, pl.ds(pl.multiple_of(c * COLS, COLS), COLS)], wdb.at[slot], d_sem.at[slot])
+        for which, w in enumerate((wg_hbm, wu_hbm)):
+            for j in range(2):
+                ring_copy(w.at[e, rows, pl.ds(j * wide, wide)], (item + which) % SLOTS, j).start()
+
+    def start_down(c, e, item):
+        cols = pl.ds(pl.multiple_of(c * wide, wide), wide)
+        for j in range(2):
+            ring_copy(wd_hbm.at[e, pl.ds(j * kw, kw), cols], item % SLOTS, j).start()
+
+    def wait_slot(slot):
+        for j in range(2):
+            ring_copy(wd_hbm.at[0, pl.ds(j * kw, kw), pl.ds(0, wide)], slot, j).wait()
 
     for kc in range(KCHUNKS):
         x_copy(kc).start()
-    for item in range(WSLOTS):
-        for copy in w_copies(item):
-            copy.start()
+    for step in range(SLOTS // 2):
+        start_gate(step // n_exp, step % n_exp, 2 * step)
+
+    table[...] = jnp.zeros_like(table)
+    mine = pl.ds(pl.multiple_of(core * tok_dev, tok_dev), tok_dev)
+    table[mine, 0:top_k] = route_ref[...].astype(F32)
+    table[mine, top_k:2 * top_k] = gate_ref[...]
+    comb_in[...] = table[...].T[0:2 * top_k, :]
 
     barrier = pltpu.get_barrier_semaphore()
     for off in range(1, n):
@@ -100,8 +114,6 @@
         comb_copies.append(copy)
     comb[me] = comb_in[...]
     send_own(1)
-
-    acc[...] = jnp.zeros_like(acc)
 
     for off in range(1, n):
         src = (me + off) % n
@@ -126,34 +138,41 @@
         codes[c, 0:n_exp, :] = code
         codes[c, n_exp:2 * n_exp, :] = gates
 
-    def tables(e, carry):
+    def gather_tables(e, carry):
         slot_row = lax.broadcasted_iota(jnp.int32, (half_slot, lanes), 0).astype(F32)
+        for c in range(chips):
+            code = jnp.broadcast_to(codes[c, pl.ds(e, 1), :], (half_slot, lanes))
+            pmat[e, c // 2, :, (c % 2) * lanes:(c % 2 + 1) * lanes] = jnp.where(code == slot_row, 1.0, 0.0).astype(BF16)
+        return carry
+
+    def scatter_tables(e, carry):
         slot_col = lax.broadcasted_iota(jnp.int32, (lanes, half_slot), 1).astype(F32)
         for c in range(chips):
             code = jnp.broadcast_to(codes[c, pl.ds(e, 1), :], (half_slot, lanes))
-            pmat[e, c // 2, :, (c % 2) * lanes:(c % 2 + 1) * lanes] = jnp.where(code == slot_row, 1.0, 0.0).astype(BF16)
-            smat[e, c // 2, (c % 2) * lanes:(c % 2 + 1) * lanes, :] = jnp.where(code.T == slot_col, 1.0, 0.0).astype(BF16)
+            smat[e, c * lanes:(c + 1) * lanes, :] = jnp.where(code.T == slot_col, 1.0, 0.0).astype(BF16)
             gate = jnp.broadcast_to(codes[c, pl.ds(n_exp + e, 1), :], (lanes, lanes))
             gmat[e, c * lanes:(c + 1) * lanes, :] = gate.T
         return carry
 
     relay_near(0)
     send_own(2)
-    lax.fori_loop(0, n_exp, tables, 0)
+    lax.fori_loop(0, n_exp, gather_tables, 0)
     relay_far(0)
+    lax.fori_loop(0, n_exp, scatter_tables, 0)
     gathered(0)
 
     def expert_chunk(kc, e):
-        item = kc * n_exp + e
-        slot = item % WSLOTS
-        for copy in w_copies(item):
-            copy.wait()
+        step = kc * n_exp + e
+        g_slot, u_slot = (2 * step) % SLOTS, (2 * step + 1) % SLOTS
+        wait_slot(g_slot)
+        wait_slot(u_slot)
         rows = [jnp.dot(pmat[e, h], xbuf[kc, h * half_tok:(h + 1) * half_tok, :], preferred_element_type=F32) for h in range(2)]
         xs = jnp.concatenate(rows, axis=0).astype(BF16)
         for c in range(d_ff // 256):
             cols = slice(c * 256, (c + 1) * 256)
-            g = jnp.dot(xs, wgb[slot, :, cols], preferred_element_type=F32)
-            u = jnp.dot(xs, wub[slot, :, cols], preferred_element_type=F32)
+            j, at = c * 256 // wide, c * 256 % wide
+            g = jnp.dot(xs, ring[g_slot, j * kw:(j + 1) * kw, at:at + 256], preferred_element_type=F32)
+            u = jnp.dot(xs, ring[u_slot, j * kw:(j + 1) * kw, at:at + 256], preferred_element_type=F32)
             if kc > 0:
                 g = gacc[e, :, cols] + g
                 u = uacc[e, :, cols] + u
@@ -163,29 +182,31 @@
             else:
                 hid[e, :, cols] = (jax.nn.silu(g) * u).astype(BF16)
 
-        @pl.when(item + WSLOTS < n_items)
-        def _():
-            for copy in w_copies(item + WSLOTS):
-                copy.start()
+        nxt = 2 * step + SLOTS
+
+        @pl.when(nxt < n_gate)
+        def _():
+            start_gate(nxt // 2 // n_exp, nxt // 2 % n_exp, nxt)
+
+        @pl.when((nxt >= n_gate) & (nxt < n_items))
+        def _():
+            for i in range(2):
+                start_down((nxt + i - n_gate) // n_exp, (nxt + i - n_gate) % n_exp, nxt + i)
 
     for kc in range(KCHUNKS):
         def body(e, carry, kc=kc):
             expert_chunk(kc, e)
             nxt = kc + 1
             if nxt < KCHUNKS:
-                @pl.when(e == 1)
+                @pl.when(e == 0)
                 def _():
                     relay_near(nxt)
                     if nxt + 2 < KCHUNKS:
                         send_own(nxt + 2)
 
-                @pl.when(e == n_exp - 3)
+                @pl.when(e == n_exp // 2)
                 def _():
                     relay_far(nxt)
-            else:
-                @pl.when(e < DSLOTS)
-                def _():
-                    d_copy(e).start()
             return carry
 
         lax.fori_loop(0, n_exp, body, 0)
@@ -196,59 +217,81 @@
         return remote(acc.at[c, :, other], sib.at[c], rs_send.at[0, c], rs_recv.at[0, c], sibling)
 
     def far_right(c):
-        return remote(red.at[c, c_opp, :, pl.ds(0, COLS // 2)], ra.at[c], rs_send.at[1, c], rs_recv.at[1, c], right)
+        return remote(acc.at[c, c_opp, core, :, pl.ds(0, COLS // 2)], ra.at[c], rs_send.at[1, c], rs_recv.at[1, c], right)
 
     def far_left(c):
-        return remote(red.at[c, c_opp, :, pl.ds(COLS // 2, COLS // 2)], rb.at[c], rs_send.at[2, c], rs_recv.at[2, c], left)
+        return remote(acc.at[c, c_opp, core, :, pl.ds(COLS // 2, COLS // 2)], rb.at[c], rs_send.at[2, c], rs_recv.at[2, c], left)
 
     def near_right(c):
-        return remote(red.at[c, c_right], rl.at[c], rs_send.at[3, c], rs_recv.at[3, c], right)
+        return remote(acc.at[c, c_right, core], rl.at[c], rs_send.at[3, c], rs_recv.at[3, c], right)
 
     def near_left(c):
-        return remote(red.at[c, c_left], rr.at[c], rs_send.at[4, c], rs_recv.at[4, c], left)
+        return remote(acc.at[c, c_left, core], rr.at[c], rs_send.at[4, c], rs_recv.at[4, c], left)
 
     def stage2(c):
         to_sibling(c).wait_recv()
-        red[c] = acc[c, :, core] + sib[c]
+        acc[c, :, core] = acc[c, :, core] + sib[c]
         far_right(c).start()
         far_left(c).start()
 
     def stage3(c):
         far_right(c).wait_recv()
-        red[c, c_right, :, :COLS // 2] = red[c, c_right, :, :COLS // 2] + ra[c]
+        acc[c, c_right, core, :, :COLS // 2] = acc[c, c_right, core, :, :COLS // 2] + ra[c]
         near_right(c).start()
         far_left(c).wait_recv()
-        red[c, c_left, :, COLS // 2:] = red[c, c_left, :, COLS // 2:] + rb[c]
+        acc[c, c_left, core, :, COLS // 2:] = acc[c, c_left, core, :, COLS // 2:] + rb[c]
         near_left(c).start()
 
     def stage4(c):
         near_right(c).wait_recv()
         near_left(c).wait_recv()
-        y_ref[:, pl.ds(pl.multiple_of(c * COLS, COLS), COLS)] = (red[c, chip] + rl[c] + rr[c]).astype(BF16)
+        y_ref[:, pl.ds(pl.multiple_of(c * COLS, COLS), COLS)] = (acc[c, chip, core] + rl[c] + rr[c]).astype(BF16)
+
+    per = wide // COLS
+
+    def down_item(c, e):
+        return n_gate + (c // per) * n_exp + e
 
     def down(c):
-        slot = c % DSLOTS
-        d_copy(c).wait()
+        cols = pl.ds(pl.multiple_of((c % per) * COLS, COLS), COLS)
         for e in range(n_exp):
-            out = jnp.dot(hid[e], wdb[slot, e], preferred_element_type=F32).astype(BF16)
-            for ch in range(chips):
-                h, rows = ch // 2, slice((ch % 2) * lanes, (ch % 2 + 1) * lanes)
-                put = jnp.dot(smat[e, h, rows, :], out[h * half_slot:(h + 1) * half_slot], preferred_element_type=F32)
+            slot = down_item(c, e) % SLOTS
+
+            @pl.when(c % per == 0)
+            def _():
+                wait_slot(slot)
+        for e in range(n_exp):
+            slot = down_item(c, e) % SLOTS
+            outs[e] = jnp.dot(hid[e], ring[slot, :, cols], preferred_element_type=F32).astype(BF16)
+
+    def put_back(c):
+        for ch in range(chips):
+            total = None
+            for e in range(n_exp):
+                put = jnp.dot(smat[e, ch * lanes:(ch + 1) * lanes, :], outs[e, (ch // 2) * half_slot:(ch // 2 + 1) * half_slot, :],
+                              preferred_element_type=F32)
                 gate = gmat[e, ch * lanes:(ch + 1) * lanes, :]
                 put = put * jnp.concatenate([gate] * (COLS // lanes), axis=1)
-                acc[c, ch] = acc[c, ch] + put.reshape(2, tok_dev, COLS)
-
-        @pl.when(c + DSLOTS < n_chunks)
-        def _():
-            d_copy(c + DSLOTS).start()
+                total = put if total is None else total + put
+            acc[c, ch] = total.reshape(2, tok_dev, COLS)
+
+        @pl.when(c % per == per - 1)
+        def _():
+            for e in range(n_exp):
+                nxt = down_item(c, e) + SLOTS
+
+                @pl.when(nxt < n_items)
+                def _():
+                    start_down((nxt - n_gate) // n_exp, (nxt - n_gate) % n_exp, nxt)
 
     def chunk_body(c, carry):
         down(c)
+
+        @pl.when(c >= 1)
+        def _():
+            stage2(c - 1)
+        put_back(c)
         to_sibling(c).start()
-
-        @pl.when(c >= 1)
-        def _():
-            stage2(c - 1)
 
         @pl.when(c >= 2)
         def _():
@@ -299,33 +342,28 @@
         n_chunks = d_model // COLS
         dims = (n, tok_dev, d_model, d_ff, n_exp, top_k, cap)
 
-        table = jnp.concatenate([route.astype(F32).T, gate.T], axis=0)
-        mine = lax.broadcasted_iota(jnp.int32, (1, lanes), 1) // tok_dev == lax.axis_index("ep") % 2
-        empty = jnp.where(lax.broadcasted_iota(jnp.int32, (2 * top_k, 1), 0) < top_k, 0.0, 0.0)
-        table = jnp.where(mine, jnp.concatenate([table, table], axis=1), empty)
-
         hbm = pl.BlockSpec(memory_space=pl.ANY)
         vmem = pl.BlockSpec(memory_space=pltpu.VMEM)
         return pl.pallas_call(
             functools.partial(moe_kernel, dims),
             out_shape=jax.ShapeDtypeStruct((tok_dev, d_model), BF16),
-            in_specs=[hbm, vmem, hbm, hbm, hbm],
+            in_specs=[hbm, vmem, vmem, hbm, hbm, hbm],
             out_specs=vmem,
             scratch_shapes=[
                 pltpu.VMEM((KCHUNKS, n * tok_dev, kw), BF16),
+                pltpu.VMEM((lanes, lanes), F32),
+                pltpu.VMEM((2 * top_k, lanes), F32),
                 pltpu.VMEM((n, 2 * top_k, lanes), F32),
                 pltpu.VMEM((chips, 2 * n_exp, lanes), F32),
                 pltpu.VMEM((n_exp, 2, n * cap // 2, n * tok_dev // 2), BF16),
-                pltpu.VMEM((n_exp, 2, n * tok_dev // 2, n * cap // 2), BF16),
+                pltpu.VMEM((n_exp, n * tok_dev, n * cap // 2), BF16),
                 pltpu.VMEM((n_exp, n * tok_dev, lanes), F32),
                 pltpu.VMEM((n_exp, n * cap, d_ff), F32),
                 pltpu.VMEM((n_exp, n * cap, d_ff), F32),
                 pltpu.VMEM((n_exp, n * cap, d_ff), BF16),
-                pltpu.VMEM((WSLOTS, kw, d_ff), BF16),
-                pltpu.VMEM((WSLOTS, kw, d_ff), BF16),
-                pltpu.VMEM((DSLOTS, n_exp, d_ff, COLS), BF16),
+                pltpu.VMEM((SLOTS, 2 * kw, d_ff // 2), BF16),
+                pltpu.VMEM((n_exp, n * cap, COLS), BF16),
                 pltpu.VMEM((n_chunks, chips, 2, tok_dev, COLS), F32),
-                pltpu.VMEM((n_chunks, chips, tok_dev, COLS), F32),
                 pltpu.VMEM((n_chunks, chips, tok_dev, COLS), F32),
                 pltpu.VMEM((n_chunks, tok_dev, COLS // 2), F32),
                 pltpu.VMEM((n_chunks, tok_dev, COLS // 2), F32),
@@ -336,12 +374,11 @@
                 pltpu.SemaphoreType.DMA((n,)),
                 pltpu.SemaphoreType.DMA((KCHUNKS, 7)),
                 pltpu.SemaphoreType.DMA((KCHUNKS, n)),
-                pltpu.SemaphoreType.DMA((WSLOTS, 2)),
-                pltpu.SemaphoreType.DMA((DSLOTS,)),
+                pltpu.SemaphoreType.DMA((SLOTS, 2)),
                 pltpu.SemaphoreType.DMA((5, n_chunks)),
                 pltpu.SemaphoreType.DMA((5, n_chunks)),
             ],
             compiler_params=pltpu.CompilerParams(collective_id=0, has_side_effects=True, vmem_limit_bytes=67_043_328),
-        )(tok, table, wg, wu, wd)
+        )(tok, route, gate, wg, wu, wd)
 
     return jax.shard_map(local_step, mesh=mesh, in_specs=(row_spec, row_spec, row_spec, expert_spec, expert_spec, expert_spec), out_specs=row_spec, check_vma=False)

time: 93.3 us -> 89 us (0.954)
  Pallas kernels: 89.3 us -> 84.4 us
  local copies, waits for them, and re-layouts: 1.67 us -> 4.42 us
  other arithmetic: 2.13 us -> 0 us
    pallas_call x1, Pallas kernels: 89.3 us -> 84.4 us  [local_step(): pl.pallas_call(functools.partial(moe_kernel, dims), out_shape=jax.ShapeDt...]
    unnamed x1 -> x3, local copies, waits for them, and re-layouts: 1.67 us -> 4.42 us
    select_n x1 -> x0, other arithmetic: 1.44 us -> none  [local_step(): table = jnp.where(mine, jnp.concatenate([table, table], axis=1), empty)]
where the time goes in v2:
time: 89 us; the launch traced here: 88.8 us
  Pallas kernels  84.4 us (95%)
  local copies, waits for them, and re-layouts  4.42 us (5%)
    pallas_call x1, Pallas kernels, local_step(): pl.pallas_call(functools.partial(moe_kernel, dims), out_shape=jax.ShapeDt...  84.4 us
    unnamed x3, local copies, waits for them, and re-layouts  4.42 us

profile of v2, /device:TPU:112, one launch (start us, length us, event | category | flops | bytes accessed | tf_op | source)
XLA Modules:
  0.0 88.8 jit_solution(6573396199179785057)
XLA Ops:
  0.0 1.4 %copy.7.route_ref = s32[64,8]{1,0:T(8,128)} copy(s32[64,8]{0,1:T(8,128)} %param.7) | data formatting | bytes 4096 | tf_op args[1]
  1.4 1.4 %copy.8.gate_ref = f32[64,8]{1,0:T(8,128)} copy(f32[64,8]{0,1:T(8,128)} %param.8) | data formatting | bytes 4096 | tf_op args[2]
  2.8 84.4 %shard_map.64 = bf16[64,2048]{1,0:T(8,128)(2,1)} custom-call(bf16[64,2048]{1,0:T(8,128)(2,1)} %x_hbm.1, s32[64,8]{1,0:T(8,128)} %copy.7.route_ref, f32[64,8]{1,0:T(8,128)} %copy.8.gate_ref, bf16[8,2048,1024]{2,1,0:T(8,128)(2,1)} %wg_hbm.1, bf16[8,2048,1024]{2,1,0:T(8,128)(2,1)} %wu_hbm.1, bf16[8,1024,2048]{2,1,0:T(8,128)(2,1)} %wd_hbm.1), custom_call_target="tpu_custom_call" | custom-call | tf_op jit(solution)/shard_map/pallas_call | solution.py:347
  87.1 1.7 %copy.10 = bf16[64,2048]{1,0:T(8,128)(2,1)} copy(bf16[64,2048]{1,0:T(8,128)(2,1)} %shard_map.64) | data formatting | bytes 524288

commit v3 on v2

v3 whole, which is shorter than its diff:
```python
import functools

import jax
import jax.numpy as jnp
from jax import lax
from jax.experimental import pallas as pl
from jax.experimental.pallas import tpu as pltpu
from jax.sharding import PartitionSpec as P

F32 = jnp.float32
BF16 = jnp.bfloat16
KCHUNKS = 4
COLS = 256
SLOTS = 22
FILL = (4, 8, SLOTS // 2)


def moe_kernel(dims, x_hbm, route_ref, gate_ref, wg_hbm, wu_hbm, wd_hbm, y_ref,
               xbuf, comb_in, comb, codes, pmat, smat, gmat, xs, gacc, uacc, hid, ring, outs, acc, sib, ra, rb, rl, rr,
               x_sem, comb_send, comb_recv, ag_send, ag_recv, w_sem, rs_send, rs_recv):
    n, tok_dev, d_model, d_ff, n_exp, top_k, cap = dims
    chips = n // 2
    lanes = 2 * tok_dev
    kw = d_model // KCHUNKS
    n_steps = KCHUNKS * n_exp
    single = 2 * n_exp
    n_gate = 2 * n_steps
    wide = d_ff // 2
    n_items = n_gate + n_exp * (d_model // wide)
    n_chunks = d_model // COLS
    half_tok = n * tok_dev // 2
    half_slot = n * cap // 2

    me = lax.axis_index("ep")
    chip, core = me // 2, me % 2
    other = 1 - core
    sibling = chip * 2 + other
    c_right, c_left, c_opp = (chip + 1) % chips, (chip + chips - 1) % chips, (chip + 2) % chips
    right, left, opp = c_right * 2 + core, c_left * 2 + core, c_opp * 2 + core

    def remote(src, dst, send, recv, dev):
        return pltpu.make_async_remote_copy(src_ref=src, dst_ref=dst, send_sem=send, recv_sem=recv,
                                            device_id={"ep": dev}, device_id_type=pl.DeviceIdType.MESH)

    def x_copy(kc):
        return pltpu.make_async_copy(x_hbm.at[:, pl.ds(kc * kw, kw)],
                                     xbuf.at[kc, pl.ds(pl.multiple_of(me * tok_dev, tok_dev), tok_dev), :], x_sem.at[kc])

    def gate_copy(w, kc, e, slot):
        return pltpu.make_async_copy(w.at[e, pl.ds(pl.multiple_of(kc * kw, kw), kw), :], ring.at[slot], w_sem.at[slot])

    def wait_slot(slot):
        gate_copy(wg_hbm, 0, 0, slot).wait()

    def start_pair(kc, e, item):
        gate_copy(wg_hbm, kc, e, item % SLOTS).start()
        gate_copy(wu_hbm, kc, e, (item + 1) % SLOTS).start()

    def start_down(item):
        c, e, slot = (item - n_gate) // n_exp, (item - n_gate) % n_exp, item % SLOTS
        cols = pl.ds(pl.multiple_of(c * wide, wide), wide)
        for j in range(2):
            pltpu.make_async_copy(wd_hbm.at[e, pl.ds(j * kw, kw), cols], ring.at[slot, :, pl.ds(j * wide, wide)], w_sem.at[slot]).start()

    def start_step(step):
        @pl.when(step < single)
        def _():
            start_pair(step // n_exp, step % n_exp, 2 * step)

        @pl.when((step >= single) & (step < n_steps))
        def _():
            start_pair(2 + step % 2, (step - single) // 2, 2 * step)

        @pl.when((step >= n_steps) & (2 * step < n_items))
        def _():
            start_down(2 * step)
            start_down(2 * step + 1)

    def fill(part):
        for step in range(FILL[part - 1] if part else 0, FILL[part]):
            start_pair(step // n_exp, step % n_exp, 2 * step)

    for kc in range(KCHUNKS):
        x_copy(kc).start()
    fill(0)

    mine = lax.broadcasted_iota(jnp.int32, (top_k, lanes), 1) // tok_dev == core
    for i, part in enumerate((route_ref[...].astype(F32), gate_ref[...])):
        comb_in[i * top_k:(i + 1) * top_k, :] = jnp.where(mine, jnp.concatenate([part, part], axis=1), 0.0)

    barrier = pltpu.get_barrier_semaphore()
    for off in range(1, n):
        pl.semaphore_signal(barrier, inc=1, device_id={"ep": (me + off) % n}, device_id_type=pl.DeviceIdType.MESH)
    pl.semaphore_wait(barrier, n - 1)

    def blocks(kc, first, count=1):
        return xbuf.at[kc, pl.ds(pl.multiple_of(first * tok_dev, tok_dev), count * tok_dev), :]

    def ag_copy(kc, src, dev, over_chip):
        return remote(blocks(kc, src), blocks(kc, src), ag_send, ag_recv.at[kc, over_chip], dev)

    def send_own(kc):
        for dev in (right, left, opp):
            ag_copy(kc, me, dev, 0).start()
        ag_copy(kc, me, sibling, 1).start()

    def forward(kc):
        remote(blocks(kc, 0, chips - 1), blocks(kc, 0, chips - 1), ag_send, ag_recv.at[kc, 0], sibling).wait_recv()
        for src in (left, right, opp):
            ag_copy(kc, src, sibling, 1).start()

    def gathered(kc):
        remote(blocks(kc, 0, chips), blocks(kc, 0, chips), ag_send, ag_recv.at[kc, 1], sibling).wait_recv()

    x_copy(0).wait()
    send_own(0)
    for off in range(1, n):
        remote(comb_in, comb.at[me], comb_send, comb_recv, (me + off) % n).start()
    comb[me] = comb_in[...]
    for kc in range(1, KCHUNKS):
        x_copy(kc).wait()
        send_own(kc)
    fill(1)
    comb_all = remote(comb.at[pl.ds(0, n - 1)], comb.at[pl.ds(0, n - 1)], comb_send, comb_recv, sibling)
    comb_all.wait_recv()

    t_row = lax.broadcasted_iota(jnp.int32, (lanes, lanes), 0)
    t_col = lax.broadcasted_iota(jnp.int32, (lanes, lanes), 1)
    before = jnp.where((t_row < t_col) & (t_row // tok_dev == t_col // tok_dev), 1.0, 0.0).astype(BF16)
    e_id = (lax.broadcasted_iota(jnp.int32, (n_exp, lanes), 0) + me * n_exp).astype(F32)
    lane_base = ((lax.broadcasted_iota(jnp.int32, (n_exp, lanes), 1) // tok_dev) * cap).astype(F32)
    for c in range(chips):
        both = comb[2 * c] + comb[2 * c + 1]
        hits = jnp.zeros((n_exp, lanes), F32)
        gates = jnp.zeros((n_exp, lanes), F32)
        for k in range(top_k):
            same = jnp.broadcast_to(both[k:k + 1, :], (n_exp, lanes)) == e_id
            hits = hits + jnp.where(same, 1.0, 0.0)
            gates = gates + jnp.where(same, jnp.broadcast_to(both[top_k + k:top_k + k + 1, :], (n_exp, lanes)), 0.0)
        rank = jnp.dot(hits.astype(BF16), before, preferred_element_type=F32)
        code = jnp.where(hits > 0.0, rank + lane_base + float((c % 2) * 2 * cap), -1.0)
        codes[c, 0:n_exp, :] = code
        codes[c, n_exp:2 * n_exp, :] = gates

    def gather_tables(e, carry):
        slot_row = lax.broadcasted_iota(jnp.int32, (half_slot, lanes), 0).astype(F32)
        for c in range(chips):
            code = jnp.broadcast_to(codes[c, pl.ds(e, 1), :], (half_slot, lanes))
            pmat[c // 2, e, :, (c % 2) * lanes:(c % 2 + 1) * lanes] = jnp.where(code == slot_row, 1.0, 0.0).astype(BF16)
        return carry

    def scatter_tables(e):
        slot_col = lax.broadcasted_iota(jnp.int32, (lanes, half_slot), 1).astype(F32)
        for c in range(chips):
            code = jnp.broadcast_to(codes[c, pl.ds(e, 1), :], (half_slot, lanes))
            smat[e, c * lanes:(c + 1) * lanes, :] = jnp.where(code.T == slot_col, 1.0, 0.0).astype(BF16)
            gate = jnp.broadcast_to(codes[c, pl.ds(n_exp + e, 1), :], (lanes, lanes))
            gmat[e, c * lanes:(c + 1) * lanes, :] = gate.T

    lax.fori_loop(0, n_exp, gather_tables, 0)
    forward(0)
    fill(2)

    def gather(kc, g):
        gathered(kc)
        for h in range(2):
            picks = pmat[h].reshape(n_exp * half_slot, half_tok)
            for at in range(0, kw, 256):
                rows = jnp.dot(picks, xbuf[kc, h * half_tok:(h + 1) * half_tok, at:at + 256], preferred_element_type=F32)
                xs[g, :, h, :, at:at + 256] = rows.astype(BF16).reshape(n_exp, half_slot, 256)

    def expert_pass(e, slots, groups, first, last):
        for at in range(0, d_ff, 256):
            cols = slice(at, at + 256)
            g = u = None
            for i in range(groups):
                rows = xs[i, e].reshape(2 * half_slot, kw)
                dg = jnp.dot(rows, ring[slots[2 * i], :, cols], preferred_element_type=F32)
                du = jnp.dot(rows, ring[slots[2 * i + 1], :, cols], preferred_element_type=F32)
                g, u = (dg, du) if g is None else (g + dg, u + du)
            if not first:
                g = gacc[e, :, cols] + g
                u = uacc[e, :, cols] + u
            if last:
                hid[e, :, cols] = (jax.nn.silu(g) * u).astype(BF16)
            else:
                gacc[e, :, cols] = g
                uacc[e, :, cols] = u

    def take(step, count):
        slots = [(2 * step + i) % SLOTS for i in range(2 * count)]
        for slot in slots:
            wait_slot(slot)
        return slots

    def refill(step, count):
        for i in range(count):
            start_step(step + i + SLOTS // 2)

    for kc in range(2):
        def pair_body(i, carry, kc=kc):
            step = kc * n_exp + 2 * i
            slots = take(step, 2)
            for j in range(2):
                if kc == 0:
                    scatter_tables(2 * i + j)
                expert_pass(2 * i + j, slots[2 * j:2 * j + 2], 1, kc == 0, False)
            refill(step, 2)
            if kc == 0:
                @pl.when(i == n_exp // 2 - 2)
                def _():
                    forward(1)
            else:
                @pl.when(i == 0)
                def _():
                    forward(2)

                @pl.when(i == n_exp // 2 - 2)
                def _():
                    forward(3)
            return carry

        gather(kc, 0)
        lax.fori_loop(0, n_exp // 2, pair_body, 0)

    def last_body(e, carry):
        step = single + 2 * e
        slots = take(step, 2)
        expert_pass(e, slots, 2, False, True)
        refill(step, 2)
        return carry

    gather(2, 0)
    gather(3, 1)
    lax.fori_loop(0, n_exp, last_body, 0)

    half = COLS // 2

    def to_sibling(c):
        return remote(acc.at[c, :, other], sib.at[c], rs_send.at[0], rs_recv.at[0, c], sibling)

    def far_right(c):
        return remote(acc.at[c, c_opp, core, :, pl.ds(0, half)], ra.at[c], rs_send.at[1], rs_recv.at[1, c], right)

    def far_left(c):
        return remote(acc.at[c, c_opp, core, :, pl.ds(half, half)], rb.at[c], rs_send.at[2], rs_recv.at[2, c], left)

    def near_right(c, j):
        cols = pl.ds(j * half, half)
        return remote(acc.at[c, c_right, core, :, cols], rl.at[c, :, cols], rs_send.at[3], rs_recv.at[3, c], right)

    def near_left(c, j):
        cols = pl.ds(j * half, half)
        return remote(acc.at[c, c_left, core, :, cols], rr.at[c, :, cols], rs_send.at[4], rs_recv.at[4, c], left)

    def stage2(c):
        to_sibling(c).wait_recv()
        acc[c, :, core] = acc[c, :, core] + sib[c]
        far_right(c).start()
        far_left(c).start()
        near_right(c, 1).start()
        near_left(c, 0).start()

    def stage3(c):
        far_right(c).wait_recv()
        acc[c, c_right, core, :, :half] = acc[c, c_right, core, :, :half] + ra[c]
        near_right(c, 0).start()
        far_left(c).wait_recv()
        acc[c, c_left, core, :, half:] = acc[c, c_left, core, :, half:] + rb[c]
        near_left(c, 1).start()

    def stage4(c):
        remote(rl.at[c], rl.at[c], rs_send.at[3], rs_recv.at[3, c], right).wait_recv()
        remote(rr.at[c], rr.at[c], rs_send.at[4], rs_recv.at[4, c], left).wait_recv()
        y_ref[:, pl.ds(pl.multiple_of(c * COLS, COLS), COLS)] = (acc[c, chip, core] + rl[c] + rr[c]).astype(BF16)

    per = wide // COLS

    def down_item(c, e):
        return n_gate + (c // per) * n_exp + e

    def down(c):
        @pl.when(c % per == 0)
        def _():
            for e in range(n_exp):
                wait_slot(down_item(c, e) % SLOTS)
        for e in range(n_exp):
            slot = down_item(c, e) % SLOTS
            parts = [jnp.dot(hid[e, :, j * kw:(j + 1) * kw],
                             ring[slot, :, pl.ds(pl.multiple_of(j * wide + (c % per) * COLS, COLS), COLS)], preferred_element_type=F32)
                     for j in range(2)]
            outs[e] = (parts[0] + parts[1]).astype(BF16)

    def put_back(c):
        for ch in range(chips):
            total = None
            for e in range(n_exp):
                put = jnp.dot(smat[e, ch * lanes:(ch + 1) * lanes, :], outs[e, (ch // 2) * half_slot:(ch // 2 + 1) * half_slot, :],
                              preferred_element_type=F32)
                gate = gmat[e, ch * lanes:(ch + 1) * lanes, :]
                put = put * jnp.concatenate([gate] * (COLS // lanes), axis=1)
                total = put if total is None else total + put
            acc[c, ch] = total.reshape(2, tok_dev, COLS)

        @pl.when(c % per == per - 1)
        def _():
            for e in range(n_exp):
                nxt = down_item(c, e) + SLOTS

                @pl.when(nxt < n_items)
                def _():
                    start_down(nxt)

    def chunk_body(c, carry):
        down(c)

        @pl.when(c >= 1)
        def _():
            stage2(c - 1)
        put_back(c)
        to_sibling(c).start()

        @pl.when(c >= 2)
        def _():
            stage3(c - 2)

        @pl.when(c >= 4)
        def _():
            stage4(c - 4)
        return carry

    lax.fori_loop(0, n_chunks, chunk_body, 0)
    last = n_chunks - 1
    stage2(last)
    stage3(last - 1)
    stage4(last - 3)
    stage3(last)
    for c in range(last - 2, n_chunks):
        stage4(c)

    comb_all.wait_send()
    everything = xbuf.at[:, pl.ds(0, (2 * chips - 1) * tok_dev), :]
    remote(everything, everything, ag_send, ag_recv.at[0, 0], sibling).wait_send()
    for i, ref in enumerate((sib, ra, rb, rl, rr)):
        remote(ref, ref, rs_send.at[i], rs_recv.at[i, 0], sibling).wait_send()


def solution(mesh):
    n = mesh.shape["ep"]
    row_spec = P(("dp", "ep"))
    expert_spec = P("ep")

    def local_step(tok, route, gate, wg, wu, wd):
        tok_dev, d_model = tok.shape
        n_exp, _, d_ff = wg.shape
        top_k = route.shape[1]
        cap = tok_dev // 2
        chips = n // 2
        lanes = 2 * tok_dev
        kw = d_model // KCHUNKS
        n_chunks = d_model // COLS
        dims = (n, tok_dev, d_model, d_ff, n_exp, top_k, cap)

        hbm = pl.BlockSpec(memory_space=pl.ANY)
        vmem = pl.BlockSpec(memory_space=pltpu.VMEM)
        return pl.pallas_call(
            functools.partial(moe_kernel, dims),
            out_shape=jax.ShapeDtypeStruct((tok_dev, d_model), BF16),
            in_specs=[hbm, vmem, vmem, hbm, hbm, hbm],
            out_specs=vmem,
            scratch_shapes=[
                pltpu.VMEM((KCHUNKS, n * tok_dev, kw), BF16),
                pltpu.VMEM((2 * top_k, lanes), F32),
                pltpu.VMEM((n, 2 * top_k, lanes), F32),
                pltpu.VMEM((chips, 2 * n_exp, lanes), F32),
                pltpu.VMEM((2, n_exp, n * cap // 2, n * tok_dev // 2), BF16),
                pltpu.VMEM((n_exp, n * tok_dev, n * cap // 2), BF16),
                pltpu.VMEM((n_exp, n * tok_dev, lanes), F32),
                pltpu.VMEM((2, n_exp, 2, n * cap // 2, kw), BF16),
                pltpu.VMEM((n_exp, n * cap, d_ff), F32),
                pltpu.VMEM((n_exp, n * cap, d_ff), F32),
                pltpu.VMEM((n_exp, n * cap, d_ff), BF16),
                pltpu.VMEM((SLOTS, kw, d_ff), BF16),
                pltpu.VMEM((n_exp, n * cap, COLS), BF16),
                pltpu.VMEM((n_chunks, chips, 2, tok_dev, COLS), F32),
                pltpu.VMEM((n_chunks, chips, tok_dev, COLS), F32),
                pltpu.VMEM((n_chunks, tok_dev, COLS // 2), F32),
                pltpu.VMEM((n_chunks, tok_dev, COLS // 2), F32),
                pltpu.VMEM((n_chunks, tok_dev, COLS), F32),
                pltpu.VMEM((n_chunks, tok_dev, COLS), F32),
                pltpu.SemaphoreType.DMA((KCHUNKS,)),
                pltpu.SemaphoreType.DMA,
                pltpu.SemaphoreType.DMA,
                pltpu.SemaphoreType.DMA,
                pltpu.SemaphoreType.DMA((KCHUNKS, 2)),
                pltpu.SemaphoreType.DMA((SLOTS,)),
                pltpu.SemaphoreType.DMA((5,)),
                pltpu.SemaphoreType.DMA((5, n_chunks)),
            ],
            compiler_params=pltpu.CompilerParams(collective_id=0, has_side_effects=True, vmem_limit_bytes=67_043_328),
        )(tok, route.T, gate.T, wg, wu, wd)

    return jax.shard_map(local_step, mesh=mesh, in_specs=(row_spec, row_spec, row_spec, expert_spec, expert_spec, expert_spec), out_specs=row_spec, check_vma=False)
```

time: 89 us -> 67.5 us (0.76)
  Pallas kernels: 84.4 us -> 65.7 us
  local copies, waits for them, and re-layouts: 4.42 us -> 1.67 us
    pallas_call x1, Pallas kernels: 84.4 us -> 65.7 us  [local_step(): pl.pallas_call(functools.partial(moe_kernel, dims), out_shape=jax.ShapeDt...]
    unnamed x3 -> x1, local copies, waits for them, and re-layouts: 4.42 us -> 1.67 us
where the time goes in v3:
time: 67.5 us; the launch traced here: 67.3 us
  Pallas kernels  65.7 us (97%)
  local copies, waits for them, and re-layouts  1.67 us (2%)
    pallas_call x1, Pallas kernels, local_step(): pl.pallas_call(functools.partial(moe_kernel, dims), out_shape=jax.ShapeDt...  65.7 us
    unnamed x1, local copies, waits for them, and re-layouts  1.67 us

profile of v3, /device:TPU:112, one launch (start us, length us, event | category | flops | bytes accessed | tf_op | source)
XLA Modules:
  0.0 67.3 jit_solution(9388683928078594369)
XLA Ops:
  0.0 65.7 %shard_map.64 = bf16[64,2048]{1,0:T(8,128)(2,1)} custom-call(bf16[64,2048]{1,0:T(8,128)(2,1)} %x_hbm.1, s32[8,64]{1,0:T(8,128)} %bitcast.2, f32[8,64]{1,0:T(8,128)} %bitcast.3, bf16[8,2048,1024]{2,1,0:T(8,128)(2,1)} %wg_hbm.1, bf16[8,2048,1024]{2,1,0:T(8,128)(2,1)} %wu_hbm.1, bf16[8,1024,2048]{2,1,0:T(8,128)(2,1)} %wd_hbm.1), custom_call_target="tpu_custom_call" | custom-call | tf_op jit(solution)/shard_map/pallas_call | solution.py:366
  65.7 1.7 %copy.8 = bf16[64,2048]{1,0:T(8,128)(2,1)} copy(bf16[64,2048]{1,0:T(8,128)(2,1)} %shard_map.64) | data formatting | bytes 524288

commit v4 on v3

--- a/solution.py
+++ b/solution.py
@@ -112,17 +112,26 @@
     def gathered(kc):
         remote(blocks(kc, 0, chips), blocks(kc, 0, chips), ag_send, ag_recv.at[kc, 1], sibling).wait_recv()
 
+    def table_copy(i, dev):
+        rows = pl.ds(i * top_k, top_k)
+        return remote(comb_in.at[rows, :], comb.at[me, rows, :], comb_send.at[i], comb_recv.at[i], dev)
+
+    def table_all(i):
+        part = comb.at[pl.ds(0, n - 1), pl.ds(i * top_k, top_k), :]
+        return remote(part, part, comb_send.at[i], comb_recv.at[i], sibling)
+
+    for off in range(1, n):
+        table_copy(0, (me + off) % n).start()
+    comb[me] = comb_in[...]
     x_copy(0).wait()
     send_own(0)
     for off in range(1, n):
-        remote(comb_in, comb.at[me], comb_send, comb_recv, (me + off) % n).start()
-    comb[me] = comb_in[...]
+        table_copy(1, (me + off) % n).start()
     for kc in range(1, KCHUNKS):
         x_copy(kc).wait()
         send_own(kc)
     fill(1)
-    comb_all = remote(comb.at[pl.ds(0, n - 1)], comb.at[pl.ds(0, n - 1)], comb_send, comb_recv, sibling)
-    comb_all.wait_recv()
+    table_all(0).wait_recv()
 
     t_row = lax.broadcasted_iota(jnp.int32, (lanes, lanes), 0)
     t_col = lax.broadcasted_iota(jnp.int32, (lanes, lanes), 1)
@@ -130,17 +139,22 @@
     e_id = (lax.broadcasted_iota(jnp.int32, (n_exp, lanes), 0) + me * n_exp).astype(F32)
     lane_base = ((lax.broadcasted_iota(jnp.int32, (n_exp, lanes), 1) // tok_dev) * cap).astype(F32)
     for c in range(chips):
-        both = comb[2 * c] + comb[2 * c + 1]
+        route = comb[2 * c, 0:top_k] + comb[2 * c + 1, 0:top_k]
         hits = jnp.zeros((n_exp, lanes), F32)
-        gates = jnp.zeros((n_exp, lanes), F32)
         for k in range(top_k):
-            same = jnp.broadcast_to(both[k:k + 1, :], (n_exp, lanes)) == e_id
-            hits = hits + jnp.where(same, 1.0, 0.0)
-            gates = gates + jnp.where(same, jnp.broadcast_to(both[top_k + k:top_k + k + 1, :], (n_exp, lanes)), 0.0)
+            hits = hits + jnp.where(jnp.broadcast_to(route[k:k + 1, :], (n_exp, lanes)) == e_id, 1.0, 0.0)
         rank = jnp.dot(hits.astype(BF16), before, preferred_element_type=F32)
-        code = jnp.where(hits > 0.0, rank + lane_base + float((c % 2) * 2 * cap), -1.0)
-        codes[c, 0:n_exp, :] = code
-        codes[c, n_exp:2 * n_exp, :] = gates
+        codes[c, 0:n_exp, :] = jnp.where(hits > 0.0, rank + lane_base + float((c % 2) * 2 * cap), -1.0)
+
+    def gate_codes():
+        table_all(1).wait_recv()
+        for c in range(chips):
+            both = comb[2 * c] + comb[2 * c + 1]
+            gates = jnp.zeros((n_exp, lanes), F32)
+            for k in range(top_k):
+                same = jnp.broadcast_to(both[k:k + 1, :], (n_exp, lanes)) == e_id
+                gates = gates + jnp.where(same, jnp.broadcast_to(both[top_k + k:top_k + k + 1, :], (n_exp, lanes)), 0.0)
+            codes[c, n_exp:2 * n_exp, :] = gates
 
     def gather_tables(e, carry):
         slot_row = lax.broadcasted_iota(jnp.int32, (half_slot, lanes), 0).astype(F32)
@@ -160,6 +174,7 @@
     lax.fori_loop(0, n_exp, gather_tables, 0)
     forward(0)
     fill(2)
+    gate_codes()
 
     def gather(kc, g):
         gathered(kc)
@@ -223,16 +238,17 @@
         gather(kc, 0)
         lax.fori_loop(0, n_exp // 2, pair_body, 0)
 
-    def last_body(e, carry):
-        step = single + 2 * e
-        slots = take(step, 2)
-        expert_pass(e, slots, 2, False, True)
-        refill(step, 2)
+    def last_body(i, carry):
+        step = single + 4 * i
+        slots = take(step, 4)
+        for j in range(2):
+            expert_pass(2 * i + j, slots[4 * j:4 * j + 4], 2, False, True)
+        refill(step, 4)
         return carry
 
     gather(2, 0)
     gather(3, 1)
-    lax.fori_loop(0, n_exp, last_body, 0)
+    lax.fori_loop(0, n_exp // 2, last_body, 0)
 
     half = COLS // 2
 
@@ -240,18 +256,16 @@
         return remote(acc.at[c, :, other], sib.at[c], rs_send.at[0], rs_recv.at[0, c], sibling)
 
     def far_right(c):
-        return remote(acc.at[c, c_opp, core, :, pl.ds(0, half)], ra.at[c], rs_send.at[1], rs_recv.at[1, c], right)
+        return remote(acc.at[c, c_opp, core, 0], ra.at[c], rs_send.at[1], rs_recv.at[1, c], right)
 
     def far_left(c):
-        return remote(acc.at[c, c_opp, core, :, pl.ds(half, half)], rb.at[c], rs_send.at[2], rs_recv.at[2, c], left)
+        return remote(acc.at[c, c_opp, core, 1], rb.at[c], rs_send.at[2], rs_recv.at[2, c], left)
 
     def near_right(c, j):
-        cols = pl.ds(j * half, half)
-        return remote(acc.at[c, c_right, core, :, cols], rl.at[c, :, cols], rs_send.at[3], rs_recv.at[3, c], right)
+        return remote(acc.at[c, c_right, core, j], rl.at[c, j], rs_send.at[3], rs_recv.at[3, c], right)
 
     def near_left(c, j):
-        cols = pl.ds(j * half, half)
-        return remote(acc.at[c, c_left, core, :, cols], rr.at[c, :, cols], rs_send.at[4], rs_recv.at[4, c], left)
+        return remote(acc.at[c, c_left, core, j], rr.at[c, j], rs_send.at[4], rs_recv.at[4, c], left)
 
     def stage2(c):
         to_sibling(c).wait_recv()
@@ -263,16 +277,17 @@
 
     def stage3(c):
         far_right(c).wait_recv()
-        acc[c, c_right, core, :, :half] = acc[c, c_right, core, :, :half] + ra[c]
+        acc[c, c_right, core, 0] = acc[c, c_right, core, 0] + ra[c]
         near_right(c, 0).start()
         far_left(c).wait_recv()
-        acc[c, c_left, core, :, half:] = acc[c, c_left, core, :, half:] + rb[c]
+        acc[c, c_left, core, 1] = acc[c, c_left, core, 1] + rb[c]
         near_left(c, 1).start()
 
     def stage4(c):
         remote(rl.at[c], rl.at[c], rs_send.at[3], rs_recv.at[3, c], right).wait_recv()
         remote(rr.at[c], rr.at[c], rs_send.at[4], rs_recv.at[4, c], left).wait_recv()
-        y_ref[:, pl.ds(pl.multiple_of(c * COLS, COLS), COLS)] = (acc[c, chip, core] + rl[c] + rr[c]).astype(BF16)
+        for j in range(2):
+            y_ref[:, pl.ds(pl.multiple_of(c * COLS + j * half, half), half)] = (acc[c, chip, core, j] + rl[c, j] + rr[c, j]).astype(BF16)
 
     per = wide // COLS
 
@@ -300,7 +315,8 @@
                 gate = gmat[e, ch * lanes:(ch + 1) * lanes, :]
                 put = put * jnp.concatenate([gate] * (COLS // lanes), axis=1)
                 total = put if total is None else total + put
-            acc[c, ch] = total.reshape(2, tok_dev, COLS)
+            for j in range(2):
+                acc[c, ch, :, j] = total[:, j * half:(j + 1) * half].reshape(2, tok_dev, half)
 
         @pl.when(c % per == per - 1)
         def _():
@@ -338,7 +354,8 @@
     for c in range(last - 2, n_chunks):
         stage4(c)
 
-    comb_all.wait_send()
+    for i in range(2):
+        table_all(i).wait_send()
     everything = xbuf.at[:, pl.ds(0, (2 * chips - 1) * tok_dev), :]
     remote(everything, everything, ag_send, ag_recv.at[0, 0], sibling).wait_send()
     for i, ref in enumerate((sib, ra, rb, rl, rr)):
@@ -365,7 +382,7 @@
         vmem = pl.BlockSpec(memory_space=pltpu.VMEM)
         return pl.pallas_call(
             functools.partial(moe_kernel, dims),
-            out_shape=jax.ShapeDtypeStruct((tok_dev, d_model), BF16),
+            out_shape=pltpu.VMEM((tok_dev, d_model), BF16),
             in_specs=[hbm, vmem, vmem, hbm, hbm, hbm],
             out_specs=vmem,
             scratch_shapes=[
@@ -382,22 +399,22 @@
                 pltpu.VMEM((n_exp, n * cap, d_ff), BF16),
                 pltpu.VMEM((SLOTS, kw, d_ff), BF16),
                 pltpu.VMEM((n_exp, n * cap, COLS), BF16),
-                pltpu.VMEM((n_chunks, chips, 2, tok_dev, COLS), F32),
-                pltpu.VMEM((n_chunks, chips, tok_dev, COLS), F32),
+                pltpu.VMEM((n_chunks, chips, 2, 2, tok_dev, COLS // 2), F32),
+                pltpu.VMEM((n_chunks, chips, 2, tok_dev, COLS // 2), F32),
                 pltpu.VMEM((n_chunks, tok_dev, COLS // 2), F32),
                 pltpu.VMEM((n_chunks, tok_dev, COLS // 2), F32),
-                pltpu.VMEM((n_chunks, tok_dev, COLS), F32),
-                pltpu.VMEM((n_chunks, tok_dev, COLS), F32),
+                pltpu.VMEM((n_chunks, 2, tok_dev, COLS // 2), F32),
+                pltpu.VMEM((n_chunks, 2, tok_dev, COLS // 2), F32),
                 pltpu.SemaphoreType.DMA((KCHUNKS,)),
-                pltpu.SemaphoreType.DMA,
-                pltpu.SemaphoreType.DMA,
+                pltpu.SemaphoreType.DMA((2,)),
+                pltpu.SemaphoreType.DMA((2,)),
                 pltpu.SemaphoreType.DMA,
                 pltpu.SemaphoreType.DMA((KCHUNKS, 2)),
                 pltpu.SemaphoreType.DMA((SLOTS,)),
                 pltpu.SemaphoreType.DMA((5,)),
                 pltpu.SemaphoreType.DMA((5, n_chunks)),
             ],
-            compiler_params=pltpu.CompilerParams(collective_id=0, has_side_effects=True, vmem_limit_bytes=67_043_328),
+            compiler_params=pltpu.CompilerParams(collective_id=0, has_side_effects=True, vmem_limit_bytes=66_700_000),
         )(tok, route.T, gate.T, wg, wu, wd)
 
     return jax.shard_map(local_step, mesh=mesh, in_specs=(row_spec, row_spec, row_spec, expert_spec, expert_spec, expert_spec), out_specs=row_spec, check_vma=False)

time: 67.5 us -> 64.6 us (0.957)
  Pallas kernels: 65.7 us -> 63.7 us
  local copies, waits for them, and re-layouts: 1.67 us -> 0.71 us
    pallas_call x1, Pallas kernels: 65.7 us -> 63.7 us  [local_step(): pl.pallas_call(functools.partial(moe_kernel, dims), out_shape=pltpu.VMEM(...]
    unnamed x1, local copies, waits for them, and re-layouts: 1.67 us -> 0.71 us
where the time goes in v4:
time: 64.6 us; the launch traced here: 64.4 us
  Pallas kernels  63.7 us (99%)
  local copies, waits for them, and re-layouts  0.71 us (1%)
    pallas_call x1, Pallas kernels, local_step(): pl.pallas_call(functools.partial(moe_kernel, dims), out_shape=pltpu.VMEM(...  63.7 us

profile of v4, /device:TPU:112, one launch (start us, length us, event | category | flops | bytes accessed | tf_op | source)
XLA Modules:
  0.0 64.4 jit_solution(2673706835174351978)
XLA Ops:
  0.0 63.7 %shard_map.64 = bf16[64,2048]{1,0:T(8,128)(2,1)S(1)} custom-call(bf16[64,2048]{1,0:T(8,128)(2,1)} %x_hbm.1, s32[8,64]{1,0:T(8,128)} %bitcast.2, f32[8,64]{1,0:T(8,128)} %bitcast.3, bf16[8,2048,1024]{2,1,0:T(8,128)(2,1)} %wg_hbm.1, bf16[8,2048,1024]{2,1,0:T(8,128)(2,1)} %wu_hbm.1, bf16[8,1024,2048]{2,1,0:T(8,128)(2,1)} %wd_hbm.1), custom_call_target="tpu_custom_call" | custom-call | tf_op jit(solution)/shard_map/pallas_call | solution.py:383
  63.7 0.7 %copy.8 = bf16[64,2048]{1,0:T(8,128)(2,1)} copy(bf16[64,2048]{1,0:T(8,128)(2,1)S(1)} %shard_map.64) | data formatting | bytes 524288

commit v5 on v4

--- a/solution.py
+++ b/solution.py
@@ -269,10 +269,12 @@
 
     def stage2(c):
         to_sibling(c).wait_recv()
-        acc[c, :, core] = acc[c, :, core] + sib[c]
+        acc[c, c_opp, core] = acc[c, c_opp, core] + sib[c, c_opp]
         far_right(c).start()
         far_left(c).start()
+        acc[c, c_right, core] = acc[c, c_right, core] + sib[c, c_right]
         near_right(c, 1).start()
+        acc[c, c_left, core] = acc[c, c_left, core] + sib[c, c_left]
         near_left(c, 0).start()
 
     def stage3(c):
@@ -287,7 +289,7 @@
         remote(rl.at[c], rl.at[c], rs_send.at[3], rs_recv.at[3, c], right).wait_recv()
         remote(rr.at[c], rr.at[c], rs_send.at[4], rs_recv.at[4, c], left).wait_recv()
         for j in range(2):
-            y_ref[:, pl.ds(pl.multiple_of(c * COLS + j * half, half), half)] = (acc[c, chip, core, j] + rl[c, j] + rr[c, j]).astype(BF16)
+            y_ref[:, pl.ds(pl.multiple_of(c * COLS + j * half, half), half)] = (acc[c, chip, core, j] + sib[c, chip, j] + rl[c, j] + rr[c, j]).astype(BF16)
 
     per = wide // COLS
 
@@ -301,10 +303,12 @@
                 wait_slot(down_item(c, e) % SLOTS)
         for e in range(n_exp):
             slot = down_item(c, e) % SLOTS
-            parts = [jnp.dot(hid[e, :, j * kw:(j + 1) * kw],
-                             ring[slot, :, pl.ds(pl.multiple_of(j * wide + (c % per) * COLS, COLS), COLS)], preferred_element_type=F32)
-                     for j in range(2)]
-            outs[e] = (parts[0] + parts[1]).astype(BF16)
+            for r in range(2):
+                rows = slice(r * half_slot, (r + 1) * half_slot)
+                parts = [jnp.dot(hid[e, rows, j * kw:(j + 1) * kw],
+                                 ring[slot, :, pl.ds(pl.multiple_of(j * wide + (c % per) * COLS, COLS), COLS)], preferred_element_type=F32)
+                         for j in range(2)]
+                outs[e, rows, :] = (parts[0] + parts[1]).astype(BF16)
 
     def put_back(c):
         for ch in range(chips):
@@ -318,6 +322,7 @@
             for j in range(2):
                 acc[c, ch, :, j] = total[:, j * half:(j + 1) * half].reshape(2, tok_dev, half)
 
+    def refill_down(c):
         @pl.when(c % per == per - 1)
         def _():
             for e in range(n_exp):
@@ -335,21 +340,20 @@
             stage2(c - 1)
         put_back(c)
         to_sibling(c).start()
+        refill_down(c)
 
         @pl.when(c >= 2)
         def _():
             stage3(c - 2)
 
-        @pl.when(c >= 4)
-        def _():
-            stage4(c - 4)
         return carry
 
     lax.fori_loop(0, n_chunks, chunk_body, 0)
     last = n_chunks - 1
     stage2(last)
     stage3(last - 1)
-    stage4(last - 3)
+    for c in range(last - 2):
+        stage4(c)
     stage3(last)
     for c in range(last - 2, n_chunks):
         stage4(c)

time: 64.6 us -> 64.2 us (level)
  no operation moved by 1% of the time
where the time goes in v5:
time: 64.2 us; the launch traced here: 64.1 us
  Pallas kernels  63.3 us (99%)
  local copies, waits for them, and re-layouts  0.71 us (1%)
    pallas_call x1, Pallas kernels, local_step(): pl.pallas_call(functools.partial(moe_kernel, dims), out_shape=pltpu.VMEM(...  63.3 us

profile of v5, /device:TPU:112, one launch (start us, length us, event | category | flops | bytes accessed | tf_op | source)
XLA Modules:
  0.0 64.1 jit_solution(5135890929157520047)
XLA Ops:
  0.0 63.3 %shard_map.64 = bf16[64,2048]{1,0:T(8,128)(2,1)S(1)} custom-call(bf16[64,2048]{1,0:T(8,128)(2,1)} %x_hbm.1, s32[8,64]{1,0:T(8,128)} %bitcast.2, f32[8,64]{1,0:T(8,128)} %bitcast.3, bf16[8,2048,1024]{2,1,0:T(8,128)(2,1)} %wg_hbm.1, bf16[8,2048,1024]{2,1,0:T(8,128)(2,1)} %wu_hbm.1, bf16[8,1024,2048]{2,1,0:T(8,128)(2,1)} %wd_hbm.1), custom_call_target="tpu_custom_call" | custom-call | tf_op jit(solution)/shard_map/pallas_call | solution.py:387
  63.4 0.7 %copy.8 = bf16[64,2048]{1,0:T(8,128)(2,1)} copy(bf16[64,2048]{1,0:T(8,128)(2,1)S(1)} %shard_map.64) | data formatting | bytes 524288
